TPU v7x, 32 devices: a whole 2x2x4 slice. The times are simulated.
32 devices in a mesh: pipe: 2 (over x), tensor: 2 (over core), dp: 8 (over z, y).
Axes of the slice: x: 2, y: 2, z: 4, core: 2. Of those that a mesh axis runs over, the one named last changes fastest.
Arguments:
- attn_out: bfloat16 [2, 4, 1024, 4096], P('pipe', None, 'dp', 'tensor'), may hold values from -6 to 6
- grad_top: bfloat16 [4, 1024, 4096], P(None, 'dp', 'tensor'), may hold values from -6 to 6
- branch_grad: bfloat16 [2, 4, 1024, 4096], P('pipe', None, 'dp', 'tensor'), may hold values from -6 to 6
- error_prev: bfloat16 [2, 8, 4096, 4096], P('pipe', 'dp', 'tensor'), may hold values from -0.3984375 to 0.3984375
- q_prev: float32 [2, 4096, 64], P('pipe', 'tensor'), may hold values from -6 to 6
Outputs:
- grad_input: bfloat16 [2, 4, 1024, 4096], P('pipe', None, 'dp', 'tensor')
- error_next: bfloat16 [2, 8, 4096, 4096], P('pipe', 'dp', 'tensor')
- p_factor: float32 [2, 4096, 64], P('pipe', 'tensor')
- q_factor: float32 [2, 4096, 64], P('pipe', 'tensor')
All inputs are finite; a program needn't handle non-finite values.
Results may differ from a plain program's by a relative error of at most 0.012.
Values may be sent and summed in bfloat16 or wider, within the bound.
A program may use at most 256 MiB of HBM per device.

v0:
```python
import jax
import jax.numpy as jnp
from jax import lax
from jax.sharding import PartitionSpec as P


def from_behind(value, axis, by):
    devices = lax.axis_size(axis)
    pairs = [(i, i + by) for i in range(devices) if 0 <= i + by < devices]
    return lax.ppermute(value, axis, pairs)


def on_device(attn_out, grad_top, branch_grad, error_prev, q_prev):
    high = lax.Precision.HIGHEST
    section = lax.axis_index("pipe")
    sections = lax.axis_size("pipe")
    last = sections - 1
    micro_count = attn_out.shape[1]
    tok_rows = attn_out.shape[2]
    head_rows = attn_out.shape[3]
    width = error_prev.shape[3]
    replicas = lax.axis_size("dp")
    grads = jnp.zeros((head_rows, width), jnp.float32)
    received = jnp.zeros(grad_top.shape[1:], jnp.bfloat16)
    grad_all = jnp.zeros(grad_top.shape, jnp.bfloat16)
    for tick in range(micro_count + sections - 1):
        micro = tick - (last - section)
        valid = jnp.logical_and(micro >= 0, micro < micro_count)
        index = jnp.clip(micro, 0, micro_count - 1)
        top_slab = lax.dynamic_index_in_dim(grad_top, index, 0, keepdims=False)
        out_grad = jnp.where(section == last, top_slab, received)
        branch = lax.dynamic_index_in_dim(branch_grad[0], index, 0, keepdims=False)
        grad_in = (out_grad.astype(jnp.float32) + branch.astype(jnp.float32)).astype(jnp.bfloat16)
        updated = lax.dynamic_update_index_in_dim(grad_all, grad_in, index, 0)
        grad_all = jnp.where(valid, updated, grad_all)
        acts = lax.dynamic_index_in_dim(attn_out[0], index, 0, keepdims=False)
        contrib = lax.dot_general(
            acts,
            lax.all_gather(out_grad, "tensor", axis=1, tiled=True),
            (((0,), (0,)), ((), ())),
            preferred_element_type=jnp.float32,
        )
        grads = grads + jnp.where(valid, contrib, 0.0)
        received = from_behind(grad_in, "pipe", -1)
    matrix = grads / (micro_count * tok_rows) + error_prev[0, 0].astype(jnp.float32)
    p_local = jnp.dot(
        matrix, lax.all_gather(q_prev[0], "tensor", axis=0, tiled=True), precision=high
    )
    praw = lax.psum(p_local, "dp") / replicas
    gram = lax.psum(jnp.dot(praw.T, praw, precision=high), "tensor")
    lower = jnp.linalg.cholesky(gram)
    phat = lax.linalg.triangular_solve(lower, praw, left_side=False, lower=True, transpose_a=True)
    q_local = lax.dot_general(matrix, phat, (((0,), (0,)), ((), ())), precision=high)
    q_part = lax.psum_scatter(
        q_local.astype(jnp.bfloat16), "tensor", scatter_dimension=0, tiled=True
    )
    q_own = lax.psum(q_part, "dp").astype(jnp.float32) / replicas
    q_full = lax.all_gather(q_own.astype(jnp.bfloat16), "tensor", axis=0, tiled=True).astype(
        q_own.dtype
    )
    error_next = (matrix - jnp.dot(phat, q_full.T, precision=high)).astype(jnp.bfloat16)
    return (grad_all[None], error_next[None, None], phat[None], q_own[None])


def solution(mesh):
    return jax.shard_map(
        on_device,
        mesh=mesh,
        in_specs=(
            P("pipe", None, "dp", "tensor"),
            P(None, "dp", "tensor"),
            P("pipe", None, "dp", "tensor"),
            P("pipe", "dp", "tensor", None),
            P("pipe", "tensor", None),
        ),
        out_specs=(
            P("pipe", None, "dp", "tensor"),
            P("pipe", "dp", "tensor", None),
            P("pipe", "tensor", None),
            P("pipe", "tensor", None),
        ),
        check_vma=False,
    )
```

profile of v0, /device:TPU:0, one launch (start us, length us, event | category | flops | bytes accessed | tf_op | source)
XLA Modules:
  0.0 469.0 jit_solution(15129772016837344065)
XLA Ops:
  7.2 0.0 all-gather.17.cloned.1.call-start
  7.2 2.3 fusion.3
  9.6 0.0 all-gather.9.cloned.1.call-start
  9.7 1.3 collective-permute-start
  11.0 1.6 broadcast_in_dim.44
  12.5 2.2 fusion.17
  14.7 11.2 %collective-permute-done = bf16[128,2048]{1,0:T(8,128)(2,1)S(1)} collective-permute-done((bf16[128,2048]{1,0:T(8,128)(2,1)S(1)}, bf16[128,2048]{1,0:T(8,128)(2,1)S(1)}, u32[]{:S(2)}, u32[]{:S(2)}) %collective-permute-start) | collective-permute-done | bytes 524320 | tf_op jit(solution)/shard_map/ppermute | solution.py:10
  25.9 2.8 fusion.28
  28.7 0.0 all-gather.11.cloned.1.call-start
  28.7 1.3 collective-permute-start.1
  30.0 13.7 %collective-permute-done.1 = bf16[128,2048]{1,0:T(8,128)(2,1)S(1)} collective-permute-done((bf16[128,2048]{1,0:T(8,128)(2,1)S(1)}, bf16[128,2048]{1,0:T(8,128)(2,1)S(1)}, u32[]{:S(2)}, u32[]{:S(2)}) %collective-permute-start.1) | collective-permute-done | bytes 524320 | tf_op jit(solution)/shard_map/ppermute | solution.py:10
  43.8 2.8 fusion.27
  46.6 0.0 all-gather.13.cloned.1.call-start
  46.6 1.3 collective-permute-start.2
  47.9 12.9 %collective-permute-done.2 = bf16[128,2048]{1,0:T(8,128)(2,1)S(1)} collective-permute-done((bf16[128,2048]{1,0:T(8,128)(2,1)S(1)}, bf16[128,2048]{1,0:T(8,128)(2,1)S(1)}, u32[]{:S(2)}, u32[]{:S(2)}) %collective-permute-start.2) | collective-permute-done | bytes 524320 | tf_op jit(solution)/shard_map/ppermute | solution.py:10
  60.8 0.8 copy-done.3
  61.6 3.0 fusion.26
  64.6 0.0 all-gather.15.cloned.1.call-start
  64.6 1.3 collective-permute-start.3
  65.9 3.2 copy.16
  69.1 8.8 %collective-permute-done.3 = bf16[128,2048]{1,0:T(8,128)(2,1)S(1)} collective-permute-done((bf16[128,2048]{1,0:T(8,128)(2,1)S(1)}, bf16[128,2048]{1,0:T(8,128)(2,1)S(1)}, u32[]{:S(2)}, u32[]{:S(2)}) %collective-permute-start.3) | collective-permute-done | bytes 524320 | tf_op jit(solution)/shard_map/ppermute | solution.py:10
  78.0 2.7 fusion.15
  80.7 0.0 all-gather.19.cloned.1.call-start
  80.7 0.5 all-gather.19.cloned.1.call-update
  81.3 0.2 all-reduce.3.cloned.1.call-start
  81.5 14.7 %fusion.10 = f32[2048,4096]{1,0:T(8,128)} fusion(bf16[1,128,4096]{2,1,0:T(8,128)(2,1)} %all-gather.17.cloned.1.call-done, bf16[1,4,128,2048]{3,2,1,0:T(8,128)(2,1)S(1)} %copy-done, s32[]{:T(128)S(6)} %min.16), kind=kOutput, calls=%fused_computation.21 | convolution fusion | flops 2147483648 | bytes 35127300 | tf_op jit(solution)/shard_map/dot_general | solution.py:37
  96.3 14.3 %fusion.23 = f32[2048,4096]{1,0:T(8,128)} fusion(bf16[128,4096]{1,0:T(8,128)(2,1)} %all-gather.9.cloned.1.call-done, bf16[1,4,128,2048]{3,2,1,0:T(8,128)(2,1)S(1)} %copy-done, s32[]{:T(128)S(6)} %min.17), kind=kOutput, calls=%fused_computation.34 | convolution fusion | flops 2147483648 | bytes 35127300 | tf_op jit(solution)/shard_map/dot_general | solution.py:37
  110.6 14.4 %fusion.21 = f32[2048,4096]{1,0:T(8,128)} fusion(bf16[128,4096]{1,0:T(8,128)(2,1)} %all-gather.11.cloned.1.call-done, bf16[1,4,128,2048]{3,2,1,0:T(8,128)(2,1)S(1)} %copy-done, s32[]{:T(128)S(6)} %min.18), kind=kOutput, calls=%fused_computation.32 | convolution fusion | flops 2147483648 | bytes 35127300 | tf_op jit(solution)/shard_map/dot_general | solution.py:37
  125.0 14.3 %fusion.19 = f32[2048,4096]{1,0:T(8,128)} fusion(bf16[128,4096]{1,0:T(8,128)(2,1)} %all-gather.13.cloned.1.call-done, bf16[1,4,128,2048]{3,2,1,0:T(8,128)(2,1)S(1)} %copy-done, s32[]{:T(128)S(6)} %min.19), kind=kOutput, calls=%fused_computation.30 | convolution fusion | flops 2147483648 | bytes 35127300 | tf_op jit(solution)/shard_map/dot_general | solution.py:37
  139.3 49.4 %convert_add_fusion = f32[2048,4096]{1,0:T(8,128)} fusion(f32[2048,4096]{1,0:T(8,128)} %fusion.19, f32[2048,4096]{1,0:T(8,128)} %fusion.21, f32[2048,4096]{1,0:T(8,128)} %fusion.23, f32[2048,4096]{1,0:T(8,128)} %fusion.10, bf16[1,1,2048,4096]{3,2,1,0:T(8,128)(2,1)} %param.8, pred[]{:T(512)S(6)} %and.20, pred[]{:T(512)S(6)} %and.19, pred[]{:T(512)S(6)} %and.18, ...), kind=kOutput, calls=%fused_computation | convolution fusion | flops 2248146944 | bytes 186122256 | tf_op jit(solution)/shard_map/dot_general | solution.py:37
  188.7 37.1 %fusion.8 = f32[2048,64]{0,1:T(8,128)} fusion(f32[2048,4096]{1,0:T(8,128)} %convert_add_fusion, f32[1,4096,64]{1,2,0:T(8,128)} %all-gather.19.cloned.1.call-done), kind=kOutput, calls=%fused_computation.19 | convolution fusion | flops 6442450944 | bytes 35127296 | tf_op jit(solution)/shard_map/dot_general | solution.py:46
  225.8 0.0 reduce-scatter.2.cloned.1.call-start
  225.9 82.0 %all-reduce.3.cloned.1.call-done = f32[2048,64]{0,1:T(8,128)} async-done(((f32[2048,64]{0,1:T(8,128)}), f32[2048,64]{0,1:T(8,128)}) %all-reduce.3.cloned.1.call-update) | async-done | bytes 524304 | tf_op jit(solution)/shard_map/psum | solution.py:49
  307.9 1.8 fusion.38
  309.7 3.4 psum.22
  313.1 0.1 copy.10
  313.2 5.8 %cholesky.16 = f32[64,64]{1,0:T(8,128)S(1)} custom-call(f32[64,64]{1,0:T(8,128)S(1)} %fusion.44), custom_call_target="Cholesky" | custom-call | tf_op jit(solution)/shard_map/jit(cholesky)/cholesky | solution.py:51
  319.1 0.6 compare_reduce_fusion
  319.8 0.7 fusion.42
  320.4 4.9 %custom-call.6 = f32[1,64,64]{1,2,0:T(8,128)S(1)} custom-call(f32[1,64,64]{2,1,0:T(8,128)S(1)} %fusion.42), custom_call_target="InvertDiagBlocksLowerTriangular" | custom-call | tf_op jit(solution)/shard_map/triangular_solve | solution.py:52
  325.3 1.7 fusion.36
  327.0 26.7 %convolution_convert_fusion = bf16[4096,64]{0,1:T(8,128)(2,1)} fusion(f32[2048,4096]{1,0:T(8,128)} %convert_add_fusion, f32[2048,64]{0,1:T(8,128)S(1)} %fusion.36), kind=kOutput, calls=%fused_computation.3 | convolution fusion | flops 6442713088 | bytes 34603008 | tf_op jit(solution)/shard_map/dot_general | solution.py:53
  353.7 0.0 all-reduce.5.cloned.1.call-start
  353.8 7.2 %reduce-scatter.2.cloned.1.call-done = bf16[2048,64]{0,1:T(8,128)(2,1)} async-done(((bf16[4096,64]{0,1:T(8,128)(2,1)}), bf16[2048,64]{0,1:T(8,128)(2,1)}) %reduce-scatter.2.cloned.1.call-update) | async-done | bytes 262160 | tf_op jit(solution)/shard_map/reduce_scatter | solution.py:54
  361.0 75.5 %all-reduce.5.cloned.1.call-done = bf16[2048,64]{0,1:T(8,128)(2,1)} async-done(((bf16[2048,64]{0,1:T(8,128)(2,1)}), bf16[2048,64]{0,1:T(8,128)(2,1)}) %all-reduce.5.cloned.1.call-update) | async-done | bytes 262160 | tf_op jit(solution)/shard_map/psum | solution.py:57
  436.5 1.8 fusion.29
  438.3 2.2 all_gather.27
  440.5 22.0 %fusion = bf16[1,1,2048,4096]{3,2,1,0:T(8,128)(2,1)} fusion(f32[2048,4096]{1,0:T(8,128)} %convert_add_fusion, f32[2048,64]{0,1:T(8,128)S(1)} %fusion.36, bf16[4096,64]{0,1:T(8,128)(2,1)S(1)} %all_gather.27), kind=kOutput, calls=%fused_computation.2 | convolution fusion | flops 6459228160 | bytes 51380224 | tf_op jit(solution)/shard_map/dot_general | solution.py:61
  (23 shorter events, 0.2 us)
Async XLA Ops:
  7.2 74.3 %copy-start = (bf16[1,4,128,2048]{3,2,1,0:T(8,128)(2,1)S(1)}, bf16[1,4,128,2048]{3,2,1,0:T(8,128)(2,1)}, u32[]{:S(2)}) copy-start(bf16[1,4,128,2048]{3,2,1,0:T(8,128)(2,1)} %param.5) | copy-start | bytes 6291460
  7.2 74.3 %all-gather.17.cloned.1.call-start = ((), (), s32[]{:S(2)}) async-start(), calls=%async_computation.8 | async-start | bytes 1572864 | tf_op jit(solution)/shard_map/all_gather | solution.py:39
  9.6 86.7 %all-gather.9.cloned.1.call-start = ((), (), s32[]{:S(2)}) async-start(), calls=%async_computation.1 | async-start | bytes 1572864 | tf_op jit(solution)/shard_map/all_gather | solution.py:39
  9.7 16.2 %collective-permute-start = (bf16[128,2048]{1,0:T(8,128)(2,1)S(1)}, bf16[128,2048]{1,0:T(8,128)(2,1)S(1)}, u32[]{:S(2)}, u32[]{:S(2)}) collective-permute-start(bf16[128,2048]{1,0:T(8,128)(2,1)S(1)} %get-tuple-element.15), channel_id=1, source_target_pairs={{16,0},{17,1},{18,2},{19,3},{20,4},{21,5},{22,6},{23,7},{24,8},{25... | collective-permute-start | bytes 1572872 | tf_op jit(solution)/shard_map/ppermute | solution.py:10
  28.7 81.9 %all-gather.11.cloned.1.call-start = ((), (), s32[]{:S(2)}) async-start(), calls=%async_computation.2 | async-start | bytes 1572864 | tf_op jit(solution)/shard_map/all_gather | solution.py:39
  28.7 15.0 %collective-permute-start.1 = (bf16[128,2048]{1,0:T(8,128)(2,1)S(1)}, bf16[128,2048]{1,0:T(8,128)(2,1)S(1)}, u32[]{:S(2)}, u32[]{:S(2)}) collective-permute-start(bf16[128,2048]{1,0:T(8,128)(2,1)S(1)} %get-tuple-element.13), channel_id=1, source_target_pairs={{16,0},{17,1},{18,2},{19,3},{20,4},{21,5},{22,6},{23,7},{24,8},{25... | collective-permute-start | bytes 1572872 | tf_op jit(solution)/shard_map/ppermute | solution.py:10
  46.6 78.4 %all-gather.13.cloned.1.call-start = ((), (), s32[]{:S(2)}) async-start(), calls=%async_computation.3 | async-start | bytes 1572864 | tf_op jit(solution)/shard_map/all_gather | solution.py:39
  46.6 14.2 %collective-permute-start.2 = (bf16[128,2048]{1,0:T(8,128)(2,1)S(1)}, bf16[128,2048]{1,0:T(8,128)(2,1)S(1)}, u32[]{:S(2)}, u32[]{:S(2)}) collective-permute-start(bf16[128,2048]{1,0:T(8,128)(2,1)S(1)} %get-tuple-element.10), channel_id=1, source_target_pairs={{16,0},{17,1},{18,2},{19,3},{20,4},{21,5},{22,6},{23,7},{24,8},{25... | collective-permute-start | bytes 1572872 | tf_op jit(solution)/shard_map/ppermute | solution.py:10
  60.8 0.8 copy-start.3
  64.6 74.8 %all-gather.15.cloned.1.call-start = ((), (), s32[]{:S(2)}) async-start(), calls=%async_computation.4 | async-start | bytes 1572864 | tf_op jit(solution)/shard_map/all_gather | solution.py:39
  64.6 13.3 %collective-permute-start.3 = (bf16[128,2048]{1,0:T(8,128)(2,1)S(1)}, bf16[128,2048]{1,0:T(8,128)(2,1)S(1)}, u32[]{:S(2)}, u32[]{:S(2)}) collective-permute-start(bf16[128,2048]{1,0:T(8,128)(2,1)S(1)} %get-tuple-element.7), channel_id=1, source_target_pairs={{16,0},{17,1},{18,2},{19,3},{20,4},{21,5},{22,6},{23,7},{24,8},{25... | collective-permute-start | bytes 1572872 | tf_op jit(solution)/shard_map/ppermute | solution.py:10
  80.7 108.0 %all-gather.19.cloned.1.call-start = ((), (), s32[]{:S(2)}) async-start(), calls=%async_computation.9 | async-start | bytes 1572864 | tf_op jit(solution)/shard_map/all_gather | solution.py:47
  81.3 226.6 %all-reduce.3.cloned.1.call-start = ((), (), s32[]{:S(2)}) async-start(), calls=%async_computation.5 | async-start | bytes 1048576 | tf_op jit(solution)/shard_map/psum | solution.py:49
  225.8 135.1 %reduce-scatter.2.cloned.1.call-start = ((), (), s32[]{:S(2)}) async-start(), calls=%async_computation.6 | async-start | bytes 786432 | tf_op jit(solution)/shard_map/reduce_scatter | solution.py:54
  327.0 113.5 %copy-start.2 = (f32[2048,64]{0,1:T(8,128)}, f32[2048,64]{0,1:T(8,128)S(1)}, u32[]{:S(2)}) copy-start(f32[2048,64]{0,1:T(8,128)S(1)} %fusion.36) | copy-start | bytes 1572868
  353.7 82.8 %all-reduce.5.cloned.1.call-start = ((), (), s32[]{:S(2)}) async-start(), calls=%async_computation.7 | async-start | bytes 524288 | tf_op jit(solution)/shard_map/psum | solution.py:57
  440.5 22.0 %copy-start.1 = (bf16[1,4,128,2048]{3,2,1,0:T(8,128)(2,1)S(1)}, bf16[1,4,128,2048]{3,2,1,0:T(8,128)(2,1)}, u32[]{:S(2)}) copy-start(bf16[1,4,128,2048]{3,2,1,0:T(8,128)(2,1)} %param.5) | copy-start | bytes 6291460
Sparse Core Ops, SparseCore 0:
  10.1 11.7 all-gather.16
  28.8 10.1 all-gather.8
  46.7 9.8 all-gather.10
  64.7 9.4 all-gather.12
  80.8 9.1 all-gather.14
  91.4 10.1 all-gather.18
  226.0 81.8 all-reduce.2
  353.8 7.1 reduce-scatter.1
  364.3 72.1 all-reduce.4
where the time goes:
time: 470 us; the launch traced here: 469 us
  waiting for transfers between devices  212 us (45%)
  matrix products  196 us (42%)
  other arithmetic  29.6 us (6%)
  between operations  14 us (3%)
  starting transfers between devices  5.71 us (1%)
  local copies, waits for them, and re-layouts  5.62 us (1%)
  blocking collectives  5.57 us (1%)
    dot_general x5, matrix products, on_device(): lax.dot_general(acts, lax.all_gather(out_grad, 'tensor', axis=1, tiled=Tr...  107 us
    psum x1, waiting for transfers between devices, on_device(): praw = lax.psum(p_local, 'dp') / replicas  82 us
    psum x1, waiting for transfers between devices, on_device(): q_own = lax.psum(q_part, 'dp').astype(jnp.float32) / replicas  75.5 us
    ppermute x4, waiting for transfers between devices, from_behind(): return lax.ppermute(value, axis, pairs)  46.6 us
    dot_general x1, matrix products, on_device(): jnp.dot(matrix, lax.all_gather(q_prev[0], 'tensor', axis=0, tiled=True),...  37.1 us
    dot_general x1, matrix products, on_device(): lax.dot_general(matrix, phat, (((0,), (0,)), ((), ())), precision=high)  26.7 us
    dot_general x1, matrix products, on_device(): jnp.dot(phat, q_full.T, precision=high)  22 us
    select_n x5, other arithmetic, on_device(): grad_all = jnp.where(valid, updated, grad_all)  13.4 us
  transfers between devices with their start and end apart: 13, of which 7 were waited for; matrix products, arithmetic and copies ran while one was open for 27% of the time, Pallas kernels for 0%

commit v1 on v0

v1 whole, which is shorter than its diff:
```python
import jax
import jax.numpy as jnp
from jax import lax
from jax.sharding import PartitionSpec as P


def from_behind(value, axis, by):
    devices = lax.axis_size(axis)
    pairs = [(i, i + by) for i in range(devices) if 0 <= i + by < devices]
    return lax.ppermute(value, axis, pairs)


def add_round(a, b):
    return (a.astype(jnp.float32) + b.astype(jnp.float32)).astype(jnp.bfloat16)


def two_terms(x):
    head = x.astype(jnp.bfloat16)
    tail = (x - head.astype(jnp.float32)).astype(jnp.bfloat16)
    return head, tail


def sum_of_shares(value, axes):
    count = lax.axis_size(axes)
    rows, cols = value.shape
    pieces = value.astype(jnp.bfloat16).reshape(count, rows // count, cols)
    landed = lax.all_to_all(pieces, axes, split_axis=0, concat_axis=0, tiled=True)
    return jnp.sum(landed.astype(jnp.float32), axis=0)


def on_device(attn_out, grad_top, branch_grad, error_prev, q_prev):
    high = lax.Precision.HIGHEST
    section = lax.axis_index("pipe")
    sections = lax.axis_size("pipe")
    last = sections - 1
    micro_count, tok_rows, features = grad_top.shape
    head_rows = attn_out.shape[3]
    replicas = lax.axis_size("dp")
    tokens = micro_count * tok_rows
    branch = branch_grad[0]

    out_grads, grad_ins = [], []
    for micro in range(micro_count):
        out = grad_top[micro]
        for hop in range(sections - 1):
            if hop == 0:
                back = add_round(grad_top[micro], from_behind(branch[micro], "pipe", -1))
            else:
                back = from_behind(add_round(out, branch[micro]), "pipe", -1)
            out = jnp.where(section == last, grad_top[micro], back)
        out_grads.append(out)
        grad_ins.append(add_round(out, branch[micro]))
    grad_all = jnp.stack(grad_ins)
    out_all = lax.all_gather(jnp.concatenate(out_grads, axis=0), "tensor", axis=1, tiled=True)
    grads = lax.dot_general(
        attn_out[0].reshape(tokens, head_rows),
        out_all,
        (((0,), (0,)), ((), ())),
        preferred_element_type=jnp.float32,
    )
    matrix = (grads / tokens + error_prev[0, 0].astype(jnp.float32)).astype(jnp.bfloat16)

    rank = q_prev.shape[2]
    q_old = lax.all_gather(q_prev[0], "tensor", axis=0, tiled=True)
    p_two = jnp.dot(
        matrix, jnp.concatenate(two_terms(q_old), axis=1), preferred_element_type=jnp.float32
    )
    p_local = p_two[:, :rank] + p_two[:, rank:]
    p_rows = sum_of_shares(p_local, "dp") / replicas
    praw = lax.all_gather(p_rows, "dp", axis=0, tiled=True)
    gram = lax.psum(jnp.dot(praw.T, praw, precision=high), "tensor")
    lower = jnp.linalg.cholesky(gram)
    phat = lax.linalg.triangular_solve(lower, praw, left_side=False, lower=True, transpose_a=True)
    p_terms = jnp.concatenate(two_terms(phat), axis=1)
    q_two = lax.dot_general(
        matrix, p_terms, (((0,), (0,)), ((), ())), preferred_element_type=jnp.float32
    )
    q_local = q_two[:, :rank] + q_two[:, rank:]
    q_rows = sum_of_shares(q_local, ("tensor", "dp")) / replicas
    q_full = lax.all_gather(q_rows.astype(jnp.bfloat16), ("tensor", "dp"), axis=0, tiled=True)
    own = q_prev.shape[1]
    q_own = lax.dynamic_slice_in_dim(q_full, lax.axis_index("tensor") * own, own, 0)
    low_rank = lax.dot_general(
        p_terms,
        jnp.concatenate([q_full, q_full], axis=1),
        (((1,), (1,)), ((), ())),
        preferred_element_type=jnp.float32,
    )
    error_next = (matrix.astype(jnp.float32) - low_rank).astype(jnp.bfloat16)
    return (grad_all[None], error_next[None, None], phat[None], q_own.astype(jnp.float32)[None])


def solution(mesh):
    return jax.shard_map(
        on_device,
        mesh=mesh,
        in_specs=(
            P("pipe", None, "dp", "tensor"),
            P(None, "dp", "tensor"),
            P("pipe", None, "dp", "tensor"),
            P("pipe", "dp", "tensor", None),
            P("pipe", "tensor", None),
        ),
        out_specs=(
            P("pipe", None, "dp", "tensor"),
            P("pipe", "dp", "tensor", None),
            P("pipe", "tensor", None),
            P("pipe", "tensor", None),
        ),
        check_vma=False,
    )
```

time: 470 us -> 287 us (0.61)
  waiting for transfers between devices: 212 us -> 57.9 us
  matrix products: 196 us -> 51.1 us
  blocking collectives: 5.57 us -> 81.6 us
  local copies, waits for them, and re-layouts: 5.62 us -> 47.8 us
  other arithmetic: 29.6 us -> 24.2 us
    psum x2 -> x0, waiting for transfers between devices: 158 us -> none  [the longest x1 82 us: on_device(): praw = lax.psum(p_local, 'dp') / replicas]
    dot_general x8 -> x4, matrix products: 193 us -> 49.1 us  [the longest x1 18 us: on_device(): lax.dot_general(attn_out[0].reshape(tokens, head_rows), out_all, (((0,),...]
    all_gather x1 -> x2, blocking collectives: 2.17 us -> 63.6 us  [the longest x1 32 us: on_device(): lax.all_gather(q_rows.astype(jnp.bfloat16), ('tensor', 'dp'), axis=0, til...]
    unnamed x9 -> x14, local copies, waits for them, and re-layouts: 3.97 us -> 44 us
    all_to_all x0 -> x1, blocking collectives: none -> 14.5 us  [sum_of_shares(): lax.all_to_all(pieces, axes, split_axis=0, concat_axis=0, tiled=True)]
    select_n x5 -> x0, other arithmetic: 13.4 us -> none  [on_device(): grad_all = jnp.where(valid, updated, grad_all)]
    all_to_all x0 -> x1, waiting for transfers between devices: none -> 12.9 us  [sum_of_shares(): lax.all_to_all(pieces, axes, split_axis=0, concat_axis=0, tiled=True)]
    reduce_scatter x1 -> x0, waiting for transfers between devices: 7.22 us -> none  [on_device(): lax.psum_scatter(q_local.astype(jnp.bfloat16), 'tensor', scatter_dimensio...]
  transfers between devices with their start and end apart: 13 -> 7, of which waited for: 7 -> 5; matrix products, arithmetic and copies ran while one was open for 27% -> 12% of each run, Pallas kernels for 0% -> 0%
where the time goes in v1:
time: 287 us; the launch traced here: 286 us
  blocking collectives  81.6 us (28%)
  waiting for transfers between devices  57.9 us (20%)
  matrix products  51.1 us (18%)
  local copies, waits for them, and re-layouts  47.8 us (17%)
  other arithmetic  24.2 us (8%)
  between operations  14.3 us (5%)
  starting transfers between devices  8.81 us (3%)
    ppermute x4, waiting for transfers between devices, from_behind(): return lax.ppermute(value, axis, pairs)  45 us
    unnamed x14, local copies, waits for them, and re-layouts  44 us
    all_gather x1, blocking collectives, on_device(): lax.all_gather(q_rows.astype(jnp.bfloat16), ('tensor', 'dp'), axis=0, til...  32 us
    all_gather x1, blocking collectives, on_device(): praw = lax.all_gather(p_rows, 'dp', axis=0, tiled=True)  31.6 us
    dot_general x1, matrix products, on_device(): lax.dot_general(attn_out[0].reshape(tokens, head_rows), out_all, (((0,),...  18 us
    all_to_all x1, blocking collectives, sum_of_shares(): lax.all_to_all(pieces, axes, split_axis=0, concat_axis=0, tiled=True)  14.5 us
    all_to_all x1, waiting for transfers between devices, sum_of_shares(): lax.all_to_all(pieces, axes, split_axis=0, concat_axis=0, tiled=True)  12.9 us
    dot_general x1, matrix products, on_device(): lax.dot_general(p_terms, jnp.concatenate([q_full, q_full], axis=1), (((1,...  11.5 us
  transfers between devices with their start and end apart: 7, of which 5 were waited for; matrix products, arithmetic and copies ran while one was open for 12% of the time, Pallas kernels for 0%

profile of v1, /device:TPU:0, one launch (start us, length us, event | category | flops | bytes accessed | tf_op | source)
XLA Modules:
  0.0 285.7 jit_solution(16449809719552677688)
XLA Ops:
  7.2 0.0 copy-start
  7.2 0.0 all-gather.6.cloned.1.call-start
  7.2 2.8 slice_bitcast_fusion.3
  10.0 1.3 collective-permute-start
  11.3 1.3 collective-permute-start.1
  12.6 1.3 collective-permute-start.3
  13.9 1.3 collective-permute-start.2
  15.2 0.0 all-gather.6.cloned.1.call-update
  15.3 0.0 all-gather.4.cloned.1.call-start
  15.3 12.1 %collective-permute-done = bf16[128,2048]{1,0:T(8,128)(2,1)} collective-permute-done((bf16[128,2048]{1,0:T(8,128)(2,1)}, bf16[128,2048]{1,0:T(8,128)(2,1)}, u32[]{:S(2)}, u32[]{:S(2)}) %collective-permute-start) | collective-permute-done | bytes 524320 | tf_op jit(solution)/shard_map/ppermute | solution.py:10
  27.4 11.2 %collective-permute-done.1 = bf16[128,2048]{1,0:T(8,128)(2,1)} collective-permute-done((bf16[128,2048]{1,0:T(8,128)(2,1)}, bf16[128,2048]{1,0:T(8,128)(2,1)}, u32[]{:S(2)}, u32[]{:S(2)}) %collective-permute-start.1) | collective-permute-done | bytes 524320 | tf_op jit(solution)/shard_map/ppermute | solution.py:10
  38.6 11.2 %collective-permute-done.3 = bf16[128,2048]{1,0:T(8,128)(2,1)} collective-permute-done((bf16[128,2048]{1,0:T(8,128)(2,1)S(1)}, bf16[128,2048]{1,0:T(8,128)(2,1)}, u32[]{:S(2)}, u32[]{:S(2)}) %collective-permute-start.3) | collective-permute-done | bytes 524320 | tf_op jit(solution)/shard_map/ppermute | solution.py:10
  49.8 10.4 %collective-permute-done.2 = bf16[128,2048]{1,0:T(8,128)(2,1)} collective-permute-done((bf16[128,2048]{1,0:T(8,128)(2,1)S(1)}, bf16[128,2048]{1,0:T(8,128)(2,1)}, u32[]{:S(2)}, u32[]{:S(2)}) %collective-permute-start.2) | collective-permute-done | bytes 524320 | tf_op jit(solution)/shard_map/ppermute | solution.py:10
  60.3 5.3 %fusion.15 = (bf16[1,128,2048]{2,1,0:T(8,128)(2,1)}, bf16[128,2048]{1,0:T(8,128)(2,1)S(1)}, bf16[1,128,2048]{2,1,0:T(8,128)(2,1)}, bf16[128,2048]{1,0:T(8,128)(2...) fusion(bf16[1,4,128,2048]{3,2,1,0:T(8,128)(2,1)} %param.7, ...), kind=kLoop, calls=%fused_computation.31 | loop fusion | flops 9437184 | bytes 10485761 | tf_op jit(solution)/shard_map/stack | solution.py:53
  65.6 1.6 pad_maximum_fusion
  67.1 0.0 all-gather.4.cloned.1.call-update
  67.2 22.7 %copy.14 = bf16[1,1,2048,4096]{2,3,1,0:T(8,128)(2,1)} copy(bf16[1,1,2048,4096]{3,2,1,0:T(8,128)(2,1)} %param.8) | data formatting | bytes 33554432 | tf_op args[3]
  89.8 1.3 fusion.10
  91.2 0.0 all-gather.4.cloned.1.call-done
  91.2 0.0 copy-done
  91.2 18.0 %fusion = bf16[2048,4096]{0,1:T(8,128)(2,1)} fusion(bf16[512,4096]{1,0:T(8,128)(2,1)} %all-gather.4.cloned.1.call-done, bf16[512,2048]{1,0:T(8,128)(2,1)S(1)} %bitcast.82, bf16[1,1,2048,4096]{2,3,1,0:T(8,128)(2,1)} %copy.14), kind=kOutput, calls=%fused_computation.1 | convolution fusion | flops 8623489024 | bytes 39845888 | tf_op jit(solution)/shard_map/dot_general | solution.py:55
  109.2 8.1 %fusion.3 = f32[2048,128]{0,1:T(8,128)S(1)} fusion(bf16[2048,4096]{0,1:T(8,128)(2,1)} %fusion, bf16[4096,64]{0,1:T(8,128)(2,1)S(1)} %get-tuple-element.12, bf16[4096,64]{0,1:T(8,128)(2,1)S(1)} %get-tuple-element.13), kind=kOutput, calls=%fused_computation.8 | convolution fusion | flops 2149580800 | bytes 18874368 | tf_op jit(solution)/shard_map/dot_general | solution.py:65
  117.3 0.1 fusion.19
  117.4 14.5 %all_to_all.10 = bf16[8,256,64]{1,2,0:T(8,128)(2,1)S(1)} all-to-all(bf16[8,256,64]{1,2,0:T(8,128)(2,1)S(1)} %bitcast.85), channel_id=1, replica_groups=mesh['pipe'=2,'tensor'=2,'dp'=8] {'dp'}, dimensions={0} | all-to-all | bytes 524288 | tf_op jit(solution)/shard_map/all_to_all | solution.py:27
  132.0 31.6 %all_gather.14 = f32[2048,64]{0,1:T(8,128)S(1)} all-gather(f32[256,64]{0,1:T(8,128)S(1)} %broadcast_multiply_fusion), channel_id=1, replica_groups=mesh['pipe'=2,'tensor'=2,'dp'=8] {'dp'}, dimensions={0}, use_global_device_ids=true | all-gather | bytes 589824 | tf_op jit(solution)/shard_map/all_gather | solution.py:70
  163.6 0.6 fusion.33
  164.2 3.6 %psum.7 = f32[64,64]{0,1:T(8,128)S(1)} all-reduce(f32[64,64]{0,1:T(8,128)S(1)} %fusion.33), channel_id=1, replica_groups=mesh['pipe'=2,'tensor'=2,'dp'=8] {'tensor'}, use_global_device_ids=true, to_apply=%region_1.2 | all-reduce | flops 4096 | bytes 32768 | tf_op jit(solution)/shard_map/psum | solution.py:71
  167.7 0.1 copy.17
  167.8 5.8 %cholesky.16 = f32[64,64]{1,0:T(8,128)S(1)} custom-call(f32[64,64]{1,0:T(8,128)S(1)} %fusion.24), custom_call_target="Cholesky" | custom-call | tf_op jit(solution)/shard_map/jit(cholesky)/cholesky | solution.py:72
  173.7 0.6 compare_reduce_fusion
  174.4 0.7 fusion.21
  175.0 4.9 %custom-call.6 = f32[1,64,64]{1,2,0:T(8,128)S(1)} custom-call(f32[1,64,64]{2,1,0:T(8,128)S(1)} %fusion.21), custom_call_target="InvertDiagBlocksLowerTriangular" | custom-call | tf_op jit(solution)/shard_map/triangular_solve | solution.py:73
  179.9 1.4 fusion.32
  181.4 11.5 %fusion.20 = f32[4096,128]{0,1:T(8,128)S(1)} fusion(bf16[2048,4096]{0,1:T(8,128)(2,1)} %fusion, bf16[2048,64]{0,1:T(8,128)(2,1)S(1)} %get-tuple-element.33, bf16[2048,64]{0,1:T(8,128)(2,1)S(1)} %get-tuple-element.32), kind=kOutput, calls=%fused_computation.45 | convolution fusion | flops 2148532224 | bytes 19398656 | tf_op jit(solution)/shard_map/dot_general | solution.py:75
  192.8 0.0 copy-done.4
  192.8 0.0 copy-start.2
  192.9 0.0 copy-start.3
  192.9 0.1 fusion.2
  193.0 0.0 copy-start.5
  193.0 0.8 copy.27
  193.8 3.6 %all-to-all-start.1 = ((bf16[16,256,64]{1,2,0:T(8,128)(2,1)}), bf16[16,256,64]{1,2,0:T(8,128)(2,1)S(1)}, u32[]{:S(2)}, u32[]{:S(2)}) async-start(bf16[16,256,64]{1,2,0:T(8,128)(2,1)} %bitcast.80), calls=%async_computation.1 | async-start | bytes 1048576 | tf_op jit(solution)/shard_map/all_to_all | solution.py:27
  197.4 2.8 maximum_bitcast_fusion
  200.2 12.9 %all-to-all-done.1 = bf16[16,256,64]{1,2,0:T(8,128)(2,1)S(1)} async-done(((bf16[16,256,64]{1,2,0:T(8,128)(2,1)}), bf16[16,256,64]{1,2,0:T(8,128)(2,1)S(1)}, u32[]{:S(2)}, u32[]{:S(2)}) %all-to-all-start.1) | async-done | bytes 524320 | tf_op jit(solution)/shard_map/all_to_all | solution.py:27
  213.1 0.1 convert_reduce_fusion
  213.2 32.0 %all_gather.15 = bf16[4096,64]{0,1:T(8,128)(2,1)S(1)} all-gather(bf16[256,64]{0,1:T(8,128)(2,1)S(1)} %multiply_convert_fusion), channel_id=1, replica_groups=mesh['pipe'=2,'tensor'=2,'dp'=8] {'tensor','dp'}, dimensions={0}, use_global_device_ids=true | all-gather | bytes 557056 | tf_op jit(solution)/shard_map/all_gather | solution.py:80
  245.2 11.5 %fusion.1 = bf16[1,1,2048,4096]{2,3,1,0:T(8,128)(2,1)} fusion(bf16[2048,4096]{0,1:T(8,128)(2,1)} %fusion, bf16[4096,64]{0,1:T(8,128)(2,1)S(1)} %all_gather.15, bf16[2048,64]{0,1:T(8,128)(2,1)S(1)} %copy-done.5, bf16[2048,64]{0,1:T(8,128)(2,1)S(1)} %get-tuple-element.32), kind=kOutput, calls=%fused_computation.3 | convolution fusion | flops 2175795200 | bytes 34603008 | tf_op jit(solution)/shard_map/dot_general | solution.py:83
  256.7 0.8 bitcast_convert_fusion.1
  257.5 21.3 %copy.20 = bf16[1,1,2048,4096]{3,2,1,0:T(8,128)(2,1)} copy(bf16[1,1,2048,4096]{2,3,1,0:T(8,128)(2,1)} %fusion.1) | data formatting | bytes 33554432
  (13 shorter events, 0.1 us)
Async XLA Ops:
  7.2 84.1 %copy-start = (bf16[1,4,128,2048]{3,2,1,0:T(8,128)(2,1)S(1)}, bf16[1,4,128,2048]{3,2,1,0:T(8,128)(2,1)}, u32[]{:S(2)}) copy-start(bf16[1,4,128,2048]{3,2,1,0:T(8,128)(2,1)} %param.5) | copy-start | bytes 6291460
  7.2 82.7 %all-gather.6.cloned.1.call-start = ((), (), s32[]{:S(2)}) async-start(), calls=%async_computation.3 | async-start | bytes 1572864 | tf_op jit(solution)/shard_map/all_gather | solution.py:64
  10.0 17.3 %collective-permute-start = (bf16[128,2048]{1,0:T(8,128)(2,1)}, bf16[128,2048]{1,0:T(8,128)(2,1)}, u32[]{:S(2)}, u32[]{:S(2)}) collective-permute-start(bf16[128,2048]{1,0:T(8,128)(2,1)} %get-tuple-element.28), channel_id=1, source_target_pairs={{16,0},{17,1},{18,2},{19,3},{20,4},{21,5},{22,6},{23,7},{24,8},{25... | collective-permute-start | bytes 1572872 | tf_op jit(solution)/shard_map/ppermute | solution.py:10
  11.3 27.3 %collective-permute-start.1 = (bf16[128,2048]{1,0:T(8,128)(2,1)}, bf16[128,2048]{1,0:T(8,128)(2,1)}, u32[]{:S(2)}, u32[]{:S(2)}) collective-permute-start(bf16[128,2048]{1,0:T(8,128)(2,1)} %get-tuple-element.29), channel_id=1, source_target_pairs={{16,0},{17,1},{18,2},{19,3},{20,4},{21,5},{22,6},{23,7},{24,8},{25... | collective-permute-start | bytes 1572872 | tf_op jit(solution)/shard_map/ppermute | solution.py:10
  12.6 37.2 %collective-permute-start.3 = (bf16[128,2048]{1,0:T(8,128)(2,1)S(1)}, bf16[128,2048]{1,0:T(8,128)(2,1)}, u32[]{:S(2)}, u32[]{:S(2)}) collective-permute-start(bf16[128,2048]{1,0:T(8,128)(2,1)S(1)} %get-tuple-element.30), channel_id=1, source_target_pairs={{16,0},{17,1},{18,2},{19,3},{20,4},{21,5},{22,6},{23,7},{24,8},{25... | collective-permute-start | bytes 1572872 | tf_op jit(solution)/shard_map/ppermute | solution.py:10
  13.9 46.3 %collective-permute-start.2 = (bf16[128,2048]{1,0:T(8,128)(2,1)S(1)}, bf16[128,2048]{1,0:T(8,128)(2,1)}, u32[]{:S(2)}, u32[]{:S(2)}) collective-permute-start(bf16[128,2048]{1,0:T(8,128)(2,1)S(1)} %get-tuple-element.31), channel_id=1, source_target_pairs={{16,0},{17,1},{18,2},{19,3},{20,4},{21,5},{22,6},{23,7},{24,8},{25... | collective-permute-start | bytes 1572872 | tf_op jit(solution)/shard_map/ppermute | solution.py:10
  15.3 76.0 %all-gather.4.cloned.1.call-start = ((), (), s32[]{:S(2)}) async-start(), calls=%async_computation.2 | async-start | bytes 6291456 | tf_op jit(solution)/shard_map/all_gather | solution.py:54
  181.4 11.5 %copy-start.4 = (bf16[2048,64]{0,1:T(8,128)(2,1)}, bf16[2048,64]{0,1:T(8,128)(2,1)S(1)}, u32[]{:S(2)}) copy-start(bf16[2048,64]{0,1:T(8,128)(2,1)S(1)} %get-tuple-element.33) | copy-start | bytes 786436
  192.8 4.6 %copy-start.2 = (bf16[1,128,2048]{2,1,0:T(8,128)(2,1)S(1)}, bf16[1,128,2048]{2,1,0:T(8,128)(2,1)}, u32[]{:S(2)}) copy-start(bf16[1,128,2048]{2,1,0:T(8,128)(2,1)} %get-tuple-element.14) | copy-start | bytes 1572868
  192.9 4.6 %copy-start.3 = (bf16[1,128,2048]{2,1,0:T(8,128)(2,1)S(1)}, bf16[1,128,2048]{2,1,0:T(8,128)(2,1)}, u32[]{:S(2)}) copy-start(bf16[1,128,2048]{2,1,0:T(8,128)(2,1)} %get-tuple-element.22) | copy-start | bytes 1572868
  193.0 52.2 %copy-start.5 = (bf16[2048,64]{0,1:T(8,128)(2,1)S(1)}, bf16[2048,64]{0,1:T(8,128)(2,1)}, u32[]{:S(2)}) copy-start(bf16[2048,64]{0,1:T(8,128)(2,1)} %copy-done.4) | copy-start | bytes 786436
  193.8 19.3 %all-to-all-start.1 = ((bf16[16,256,64]{1,2,0:T(8,128)(2,1)}), bf16[16,256,64]{1,2,0:T(8,128)(2,1)S(1)}, u32[]{:S(2)}, u32[]{:S(2)}) async-start(bf16[16,256,64]{1,2,0:T(8,128)(2,1)} %bitcast.80), calls=%async_computation.1 | async-start | bytes 1048576 | tf_op jit(solution)/shard_map/all_to_all | solution.py:27
  257.5 21.3 %copy-start.1 = (bf16[1,4,128,2048]{3,2,1,0:T(8,128)(2,1)S(1)}, bf16[1,4,128,2048]{3,2,1,0:T(8,128)(2,1)}, u32[]{:S(2)}) copy-start(bf16[1,4,128,2048]{3,2,1,0:T(8,128)(2,1)} %param.5) | copy-start | bytes 6291460
Sparse Core Ops, SparseCore 0:
  15.4 16.0 all-gather.5
  67.3 14.7 all-gather.3
